TPU v7x, 32 devices: a whole 2x2x4 slice. The times are simulated.
32 devices in a mesh: win: 2 (over core), grp: 16 (over z, y, x).
Axes of the slice: x: 2, y: 2, z: 4, core: 2. Of those that a mesh axis runs over, the one named last changes fastest.
Arguments:
- atom_table: float32 [4, 6, 24576], P('win', None, 'grp'), as said below
- row_blocks: int32 [4, 1024], P('win', 'grp'), may hold values from 0 to 191, as said below
- col_blocks: int32 [4, 1024], P('win', 'grp'), may hold values from 0 to 191, as said below
- lambdas: float32 [4], replicated, may hold values from 0 to 1, as said below
- inverse_temp: float32 [1], replicated, may hold values from 20 to 80
- parity: int32 [1], replicated, may hold values from 0 to 1073741823
- thresholds: int32 [4], replicated, may hold values from 0 to 1073741823
Outputs:
- energies: float32 [4, 3], P('win')
- margins: float32 [4], P('win')
- profile: float32 [4], P('win')
Inputs may be any that keep to these rules, and one draw needn't show every extreme that they name: `row_blocks`: the first block of each pair listed on index g of grp lies in that index's share of atoms: blocks g * 12 to (g + 1) * 12 - 1. `col_blocks`: the list of one index of grp names blocks of any one index of grp (itself included) at most 5 times; in each window some index of grp has exactly 5 of its blocks named in every list of that window. `lambdas`: strictly increasing. `atom_table`: field 4 lies in 0.7 to 1.4 and field 5 in 0.6 to 1.4.
All inputs are finite; a program needn't handle non-finite values.
Results may differ from a plain program's by a relative error of at most 0.0003.
Values sent between devices are 32-bit elements; how exact they have to be, the bound alone decides.
A program may use at most 64 MiB of HBM per device.

v0:
```python
import functools

import jax
import jax.numpy as jnp
from jax import lax
from jax.experimental import pallas as pl
from jax.experimental.pallas import tpu as pltpu
from jax.sharding import PartitionSpec as P

TILE = 128
ROWS = 8
FIELDS = 6
PIECES = TILE // ROWS
MESH = pl.DeviceIdType.MESH


def grid_of(mesh):
    groups = mesh.shape["grp"]
    try:
        line = mesh.devices[0]
        coords = [tuple(d.coords) for d in line]
        dims = [len({c[a] for c in coords}) for a in (2, 1, 0)]
        base = [min(c[a] for c in coords) for a in (2, 1, 0)]
        want = [
            (base[2] + x, base[1] + y, base[0] + z)
            for z in range(dims[0])
            for y in range(dims[1])
            for x in range(dims[2])
        ]
        if [c[:3] for c in coords] == want:
            return tuple(dims)
    except Exception:
        pass
    return (groups, 1, 1)


def messages_of(dims):
    z, y, x = dims
    first = (z - 1) + (x - 1) + (y - 1)
    second = (z - 1) * (x + y - 2)
    third = z * (x - 1) * (y - 1)
    return first + second + third


def kernel(
    cfg,
    table,
    row_ids,
    col_ids,
    lambdas,
    inverse_temp,
    parity,
    thresholds,
    out_energy,
    out_margin,
    out_profile,
    *scratch,
):
    run, wins, groups, own, listed, dims = cfg
    bufs = scratch[:run]
    rowbs = scratch[run : 2 * run]
    red, send_sem, recv_sem, red_send, red_recv = scratch[2 * run :]
    dim_z, dim_y, dim_x = dims
    windows = wins * run
    win = lax.axis_index("win")
    grp = lax.axis_index("grp")
    my_z = grp // (dim_y * dim_x)
    my_y = (grp // dim_x) % dim_y
    my_x = grp % dim_x
    two_ends = wins == 2 and run == 2

    def window_of(slot):
        if two_ends:
            return jnp.where(win == 0, 1 - slot, slot)
        return slot

    def at(dz, dy, dx):
        return (
            ((my_z + dz) % dim_z) * dim_y + (my_y + dy) % dim_y
        ) * dim_x + (my_x + dx) % dim_x

    barrier = pltpu.get_barrier_semaphore()

    plane = dim_y * dim_x
    mates = wins * plane
    mate = win * plane + grp % plane

    def column_peer(dz):
        return (win, at(dz, 0, 0))

    def plane_peer(step):
        other = (mate + step) % mates
        return (other // plane, my_z * plane + other % plane)

    peers = [column_peer(dz) for dz in range(1, dim_z)]
    peers += [plane_peer(step) for step in range(1, mates)]
    for peer in peers:
        pl.semaphore_signal(barrier, inc=1, device_id=peer, device_id_type=MESH)

    def spread(slot):
        local = window_of(slot)

        def one(block, carry):
            start = pl.multiple_of(block * TILE, TILE)
            tile = table[local, :, pl.ds(start, TILE)]
            packed = jnp.concatenate(
                [tile[0:4], 4.0 * tile[4:5], 1.0 / tile[5:6], tile[0:2]], axis=0
            )
            turned = jnp.transpose(packed)
            for field in range(FIELDS):
                wide = jnp.broadcast_to(turned[:, field : field + 1], (TILE, TILE))
                for piece in range(PIECES):
                    rowbs[slot][(block * FIELDS + field) * PIECES + piece] = wide[
                        piece * ROWS : (piece + 1) * ROWS
                    ]
            return carry

        lax.fori_loop(0, own, one, 0)

    def pack(block, carry):
        start = pl.multiple_of(block * TILE, TILE)
        for slot in range(run):
            tile = table[window_of(slot), :, pl.ds(start, TILE)]
            for field in range(FIELDS):
                bufs[slot][(grp * own + block) * FIELDS + field] = tile[field : field + 1]
        return carry

    lax.fori_loop(0, own, pack, 0)

    shares = []
    lowers = []
    for wl in range(run):
        window = win * run + wl
        odd = (window + parity[0]) & 1
        lower = window - odd
        threshold = thresholds[0]
        for v in range(1, windows):
            threshold = jnp.where(lower == v, thresholds[v], threshold)
        drawn = ((threshold + parity[0]) & 1073741823) + 1
        share = jnp.full((ROWS, TILE), drawn, jnp.int32).astype(jnp.float32) * (1.0 / 1073741824.0)
        shares.append(-jnp.log(share))
        lowers.append(lower)

    pl.semaphore_wait(barrier, len(peers))

    counts = [0] * run

    def share_of(slot, owner):
        return bufs[slot].at[pl.ds(owner * (own * FIELDS), own * FIELDS)]

    def descriptor(slot, owner, target, number):
        return pltpu.make_async_remote_copy(
            src_ref=share_of(slot, owner),
            dst_ref=share_of(slot, owner),
            send_sem=send_sem.at[slot, number],
            recv_sem=recv_sem.at[slot, owner],
            device_id={"grp": target},
            device_id_type=MESH,
        )

    sent = []

    def send(slot, owner, target):
        copy = descriptor(slot, owner, target, counts[slot])
        counts[slot] += 1
        copy.start()
        sent.append(copy)

    def arrived(slot, owner):
        descriptor(slot, owner, owner, 0).wait_recv()

    def to_x(slot, owner):
        for dx in range(1, dim_x):
            send(slot, owner, at(0, 0, dx))

    def to_y(slot, owner):
        for dy in range(1, dim_y):
            send(slot, owner, at(0, dy, 0))

    def open_sends(slot):
        for dz in range(1, dim_z):
            send(slot, grp, at(dz, 0, 0))
        to_x(slot, grp)
        to_y(slot, grp)

    def pass_plane(slot, dz):
        for dx in range(1, dim_x):
            owner = at(dz, 0, dx)
            arrived(slot, owner)
            if dz % 2 == 0:
                to_y(slot, owner)
        for dy in range(1, dim_y):
            owner = at(dz, dy, 0)
            arrived(slot, owner)
            if dz % 2 == 1:
                to_x(slot, owner)

    def pass_column(slot):
        for dz in range(1, dim_z):
            owner = at(dz, 0, 0)
            arrived(slot, owner)
            to_x(slot, owner)
            to_y(slot, owner)

    def pass_planes(slot):
        for dz in range(dim_z):
            pass_plane(slot, dz)

    def last_arrivals(slot):
        for dz in range(dim_z):
            for dy in range(1, dim_y):
                for dx in range(1, dim_x):
                    arrived(slot, at(dz, dy, dx))

    def lambda_list(slot):
        window = win * run + window_of(slot)
        if two_ends and slot == 1:
            low = jnp.where(window == 0, 0, window - 1)
            return [lambdas[low], lambdas[low + 1]]
        return [
            lambdas[jnp.maximum(window - 1, 0)],
            lambdas[window],
            lambdas[jnp.minimum(window + 1, windows - 1)],
        ]

    def start_state(slot):
        zero = jnp.zeros((ROWS, TILE), jnp.float32)
        row = jnp.zeros((1, TILE), jnp.float32)
        return tuple(zero for _ in lambda_list(slot)) + (row, row)

    def tiles(slot, first, last, state):
        local = window_of(slot)
        lams = lambda_list(slot)
        cores = [1.0 - 0.5 * lam for lam in lams]
        softs = [2.0 - lam for lam in lams]
        base = grp * own

        def one(pair, state):
            row_id = row_ids[local, pair]
            col_id = col_ids[local, pair]
            first_row = col_id * FIELDS
            col = [bufs[slot][first_row + f] for f in range(FIELDS)]
            mine = jnp.clip(row_id - base, 0, own - 1) * (FIELDS * PIECES)
            fields = [jnp.broadcast_to(col[f], (ROWS, TILE)) for f in range(3)]
            charge_col = col[3]
            depth_col = col[4]
            size_col = jnp.broadcast_to(1.0 / col[5], (ROWS, TILE))
            sum_disp = [None] * len(lams)
            sum_coul = [None] * len(lams)
            for piece in range(TILE // ROWS):
                dx = rowbs[slot][mine + piece] - fields[0]
                dy = rowbs[slot][mine + 1 * PIECES + piece] - fields[1]
                dz = rowbs[slot][mine + 2 * PIECES + piece] - fields[2]
                charge = rowbs[slot][mine + 3 * PIECES + piece]
                depth = rowbs[slot][mine + 4 * PIECES + piece]
                r2 = dx * dx + dy * dy + dz * dz
                scaled = r2 * (rowbs[slot][mine + 5 * PIECES + piece] * size_col)
                cube = scaled * scaled * scaled
                for k in range(len(lams)):
                    root = lax.rsqrt(cube + cores[k])
                    inverse = root * root
                    disp = (depth * inverse) * (inverse - 1.0)
                    coul = charge * lax.rsqrt(r2 + softs[k])
                    if piece == 0:
                        sum_disp[k], sum_coul[k] = disp, coul
                    else:
                        sum_disp[k] = sum_disp[k] + disp
                        sum_coul[k] = sum_coul[k] + coul
            totals = [
                state[k] + (sum_disp[k] * depth_col + sum_coul[k] * charge_col)
                for k in range(len(lams))
            ]
            same = jnp.where(row_id == col_id, 1.0, 0.0)
            return tuple(totals) + (
                state[-2] + same * (depth_col * depth_col),
                state[-1] + same * (charge_col * charge_col),
            )

        return lax.fori_loop(first, last, one, state)

    def close(slot, state):
        out = []
        for k, lam in enumerate(lambda_list(slot)):
            core = jnp.full((1, TILE), 1.0 - 0.5 * lam, jnp.float32)
            soft = jnp.full((1, TILE), 2.0 - lam, jnp.float32)
            inverse = 1.0 / core
            own_pairs = state[-2] * (4.0 * inverse * (inverse - 1.0)) + state[-1] * lax.rsqrt(soft)
            line = jnp.sum(state[k], axis=0, keepdims=True) - own_pairs
            out.append(jnp.sum(line, axis=1, keepdims=True) * lam)
        if two_ends and slot == 1:
            out = [out[0], jnp.where(win == 0, out[0], out[1]), out[1]]
        return out

    open_sends(0)
    spread(0)
    pass_column(0)
    for slot in range(1, run):
        open_sends(slot)
    pass_planes(0)
    if run > 1:
        pass_column(1)
    for slot in range(1, run):
        spread(slot)
    last_arrivals(0)
    partial = []
    for slot in range(run):
        state = start_state(slot)
        if slot + 1 < run:
            half = (3 * listed) // 8
            state = tiles(slot, 0, half, state)
            if slot > 0:
                pass_column(slot + 1)
            pass_planes(slot + 1)
            state = tiles(slot, half, listed, state)
            last_arrivals(slot + 1)
        else:
            state = tiles(slot, 0, listed, state)
        partial.append(close(slot, state))

    lane = lax.broadcasted_iota(jnp.int32, (1, TILE), 1)
    line = jnp.zeros((1, TILE), jnp.float32)
    for slot in range(run):
        place = window_of(slot) * 3
        for k in range(3):
            line = jnp.where(lane == place + k, partial[slot][k], line)
    def copy_of(place, target, send_at, recv_at):
        return pltpu.make_async_remote_copy(
            src_ref=red.at[place],
            dst_ref=red.at[place],
            send_sem=red_send.at[send_at],
            recv_sem=red_recv.at[recv_at],
            device_id=target,
            device_id_type=MESH,
        )

    red[my_z] = line
    for dz in range(1, dim_z):
        copy_of(my_z, column_peer(dz), dz, my_z).start()
    for copy in sent:
        copy.wait_send()
    for dz in range(1, dim_z):
        place = (my_z + dz) % dim_z
        copy_of(place, column_peer(dz), dz, place).wait()
    column_sum = jnp.sum(red[0:dim_z], axis=0)
    red[dim_z + mate] = column_sum
    for step in range(1, mates):
        place = dim_z + mate
        copy_of(place, plane_peer(step), dim_z + step, place).start()
    for step in range(1, mates):
        place = dim_z + (mate + step) % mates
        copy_of(place, plane_peer(step), dim_z + step, place).wait()
    scale = 1.0 / (listed * groups * TILE * TILE)
    energy = []
    for part in range(wins):
        first = dim_z + part * plane
        total = jnp.sum(red[first : first + plane], axis=0) * scale
        for wl in range(run):
            energy.append(
                [jnp.sum(jnp.where(lane == wl * 3 + k, total, 0.0)) for k in range(3)]
            )
    ups = [e[2] - e[1] for e in energy]
    downs = [e[0] - e[1] for e in energy]
    for wl in range(run):
        window = win * run + wl
        for k in range(3):
            value = energy[wl][k]
            for part in range(1, wins):
                value = jnp.where(win == part, energy[part * run + wl][k], value)
            out_energy[wl, k] = value
        profile = jnp.float32(0.0)
        change = jnp.float32(0.0)
        for v in range(windows):
            profile = profile + jnp.where(v < window, ups[v], 0.0)
            change = change + jnp.where(lowers[wl] == v, ups[v], 0.0)
            change = change + jnp.where(lowers[wl] + 1 == v, downs[v], 0.0)
        out_profile[wl] = profile
        partner = jnp.logical_and(lowers[wl] >= 0, lowers[wl] + 1 < windows)
        margin = jnp.max(shares[wl]) - inverse_temp[0] * change
        out_margin[wl] = jnp.where(partner, margin, 0.0)


def per_device(dims, atom_table, row_blocks, col_blocks, lambdas, inverse_temp, parity, thresholds):
    run, fields, atoms = atom_table.shape
    wins = lax.axis_size("win")
    groups = lax.axis_size("grp")
    own = atoms // TILE
    listed = row_blocks.shape[1]
    cfg = (run, wins, groups, own, listed, dims)
    smem = pl.BlockSpec(memory_space=pltpu.SMEM)
    vmem = pl.BlockSpec(memory_space=pltpu.VMEM)
    places = dims[0] + wins * dims[1] * dims[2]
    scratch = [pltpu.VMEM((groups * own * fields, 1, TILE), jnp.float32) for _ in range(run)]
    scratch += [pltpu.VMEM((own * FIELDS * PIECES, ROWS, TILE), jnp.float32) for _ in range(run)]
    scratch += [
        pltpu.VMEM((places, 1, TILE), jnp.float32),
        pltpu.SemaphoreType.DMA((run, max(1, messages_of(dims)))),
        pltpu.SemaphoreType.DMA((run, groups)),
        pltpu.SemaphoreType.DMA((places,)),
        pltpu.SemaphoreType.DMA((places,)),
    ]
    return pl.pallas_call(
        functools.partial(kernel, cfg),
        out_shape=(
            jax.ShapeDtypeStruct((run, 3), jnp.float32),
            jax.ShapeDtypeStruct((run,), jnp.float32),
            jax.ShapeDtypeStruct((run,), jnp.float32),
        ),
        in_specs=[vmem, smem, smem, smem, smem, smem, smem],
        out_specs=(smem, smem, smem),
        scratch_shapes=scratch,
        compiler_params=pltpu.CompilerParams(
            collective_id=0, has_side_effects=True, vmem_limit_bytes=48 * 1024 * 1024
        ),
    )(atom_table, row_blocks, col_blocks, lambdas, inverse_temp, parity, thresholds)


def solution(mesh):
    return jax.shard_map(
        functools.partial(per_device, grid_of(mesh)),
        mesh=mesh,
        in_specs=(P("win", None, "grp"), P("win", "grp"), P("win", "grp"), P(), P(), P(), P()),
        out_specs=(P("win", None), P("win"), P("win")),
        check_vma=False,
    )
```

profile of v0, /device:TPU:0, one launch (start us, length us, event | category | flops | bytes accessed | tf_op | source)
XLA Modules:
  0.0 45.7 jit_solution(338595566439706680)
XLA Ops:
  1.9 0.0 copy-start
  1.9 0.0 copy-start.1
  1.9 0.0 copy-start.2
  2.0 0.0 copy-start.3
  2.0 0.9 %copy.10.table = f32[2,6,1536]{2,1,0:T(8,128)S(1)} copy(f32[2,6,1536]{2,0,1:T(2,128)} %param.7) | data formatting | bytes 147456 | tf_op args[0]
  2.9 0.0 copy-done
  2.9 0.0 copy-done.1
  2.9 0.0 copy-done.2
  2.9 0.0 copy-done.3
  2.9 41.1 %shard_map.94 = (f32[2,3]{1,0:T(2,128)S(1)}, f32[2]{0:T(128)S(1)}, f32[2]{0:T(128)S(1)}) custom-call(f32[2,6,1536]{2,1,0:T(8,128)S(1)} %copy.10.table, s32[2,64]{1,0:T(2,128)S(1)} %copy-done, s32[2,64]{1,0:T(2,128)S(1)} %copy-done.1, f32[4]{0:T(128)S(1)} %copy-done.2, f32[1]{0:T(128)S(6)} %copy.14.inverse_temp, s32[1]{0:T(128)S(6)} %copy.15.parity, ...), custom_call_target="tpu_custom_call" | custom-call | tf_op jit(solution)/shard_map/pallas_call | solution.py:401
  44.1 0.6 %copy.16 = f32[2,3]{1,0:T(2,128)} copy(f32[2,3]{1,0:T(2,128)S(1)} %get-tuple-element.6) | data formatting | bytes 48
  44.6 0.5 %copy.17 = f32[2]{0:T(128)} copy(f32[2]{0:T(128)S(1)} %get-tuple-element.7) | data formatting | bytes 16
  45.1 0.5 %copy.18 = f32[2]{0:T(128)} copy(f32[2]{0:T(128)S(1)} %get-tuple-element.8) | data formatting | bytes 16
Async XLA Ops:
  1.9 1.0 %copy-start = (s32[2,64]{1,0:T(2,128)S(1)}, s32[2,64]{1,0:T(2,128)}, u32[]{:S(2)}) copy-start(s32[2,64]{1,0:T(2,128)} %row_ids.1) | copy-start | bytes 1540
  1.9 1.0 %copy-start.1 = (s32[2,64]{1,0:T(2,128)S(1)}, s32[2,64]{1,0:T(2,128)}, u32[]{:S(2)}) copy-start(s32[2,64]{1,0:T(2,128)} %col_ids.1) | copy-start | bytes 1540
  1.9 1.0 %copy-start.2 = (f32[4]{0:T(128)S(1)}, f32[4]{0:T(128)}, u32[]{:S(2)}) copy-start(f32[4]{0:T(128)} %lambdas.1) | copy-start | bytes 52
  2.0 1.0 %copy-start.3 = (s32[4]{0:T(128)S(1)}, s32[4]{0:T(128)}, u32[]{:S(2)}) copy-start(s32[4]{0:T(128)} %thresholds.1) | copy-start | bytes 52
where the time goes:
time: 45.8 us; the launch traced here: 45.7 us
  Pallas kernels  41.1 us (90%)
  local copies, waits for them, and re-layouts  2.53 us (6%)
  between operations  2 us (4%)
    pallas_call x1, Pallas kernels, per_device(): pl.pallas_call(functools.partial(kernel, cfg), out_shape=(jax.ShapeDtypeS...  41.1 us
    unnamed x12, local copies, waits for them, and re-layouts  2.53 us

commit v1 on v0

v1 whole, which is shorter than its diff:
```python
import functools

import jax
import jax.numpy as jnp
from jax import lax
from jax.experimental import pallas as pl
from jax.experimental.pallas import tpu as pltpu
from jax.sharding import PartitionSpec as P

TILE = 128
ROWS = 8
FIELDS = 6
PIECES = TILE // ROWS
UNROLL = 4
LIMIT = 48 * 1024 * 1024
MESH = pl.DeviceIdType.MESH


def grid_of(mesh):
    groups = mesh.shape["grp"]
    try:
        line = mesh.devices[0]
        coords = [tuple(d.coords) for d in line]
        dims = [len({c[a] for c in coords}) for a in (2, 1, 0)]
        base = [min(c[a] for c in coords) for a in (2, 1, 0)]
        want = [
            (base[2] + x, base[1] + y, base[0] + z)
            for z in range(dims[0])
            for y in range(dims[1])
            for x in range(dims[2])
        ]
        if [c[:3] for c in coords] == want:
            return tuple(dims)
    except Exception:
        pass
    return (groups, 1, 1)


def messages_of(dims):
    z, y, x = dims
    first = (z - 1) + (x - 1) + (y - 1)
    second = (z - 1) * (x + y - 2)
    third = z * (x - 1) * (y - 1)
    return first + second + third


def split3(value):
    high = value.astype(jnp.bfloat16).astype(jnp.float32)
    rest = value - high
    middle = rest.astype(jnp.bfloat16).astype(jnp.float32)
    return high, middle, rest - middle


def kernel(
    cfg,
    table,
    row_hbm,
    col_hbm,
    lambdas_hbm,
    inverse_temp,
    parity,
    thresholds_hbm,
    out,
    *scratch,
):
    run, wins, groups, own, listed, dims = cfg
    bufs = scratch[:run]
    rowbs = scratch[run : 2 * run]
    (
        stage,
        feats,
        red,
        row_ids,
        col_ids,
        lambdas,
        thresholds,
        load_sem,
        small_sem,
        send_sem,
        recv_sem,
        red_send,
        red_recv,
        ready,
    ) = scratch[2 * run :]
    dim_z, dim_y, dim_x = dims
    windows = wins * run
    win = lax.axis_index("win")
    grp = lax.axis_index("grp")
    my_z = grp // (dim_y * dim_x)
    my_y = (grp // dim_x) % dim_y
    my_x = grp % dim_x
    two_ends = wins == 2 and run == 2
    own_pad = stage.shape[2]
    me = win * groups + grp

    def window_of(slot):
        if two_ends:
            return jnp.where(win == 0, 1 - slot, slot)
        return slot

    def lams_of(slot):
        return 2 if two_ends and slot == 1 else 3

    def fields_of(slot):
        return FIELDS + lams_of(slot)

    def group_at(z, dy, dx):
        return (z * dim_y + (my_y + dy) % dim_y) * dim_x + (my_x + dx) % dim_x

    def plane_at(step):
        places = [
            sorted(range(dim_z), key=lambda z: (abs(z - mine), z))[step]
            for mine in range(dim_z)
        ]
        chosen = places[0]
        for mine in range(1, dim_z):
            chosen = jnp.where(my_z == mine, places[mine], chosen)
        return chosen

    planes = [my_z] + [plane_at(step) for step in range(1, dim_z)]

    loads = []
    for slot in range(run):
        local = window_of(slot)
        for f in range(FIELDS):
            loads.append(
                pltpu.make_async_copy(
                    table.at[f, :, local, :],
                    bufs[slot].at[pl.ds(grp * own, own), f, 0, :],
                    load_sem.at[slot],
                )
            )
    for slot in range(run):
        local = window_of(slot)
        loads.append(
            pltpu.make_async_copy(
                table.at[:, :, local, :],
                stage.at[slot, :, pl.ds(0, own), :],
                load_sem.at[run + slot],
            )
        )
    smalls = [
        pltpu.make_async_copy(row_hbm, row_ids, small_sem.at[0]),
        pltpu.make_async_copy(col_hbm, col_ids, small_sem.at[1]),
        pltpu.make_async_copy(lambdas_hbm, lambdas, small_sem.at[2]),
        pltpu.make_async_copy(thresholds_hbm, thresholds, small_sem.at[3]),
    ]
    for copy in loads:
        copy.start()
    for copy in smalls:
        copy.start()

    barrier = pltpu.get_barrier_semaphore()
    partners = [((win + step) % wins, grp) for step in range(1, wins)]
    peers = [(win, group_at(plane, 0, 0)) for plane in planes[1:]]
    peers += [(win, group_at(my_z, 0, dx)) for dx in range(1, dim_x)]
    peers += [(win, group_at(my_z, dy, 0)) for dy in range(1, dim_y)]
    peers += partners
    for peer in peers:
        pl.semaphore_signal(barrier, inc=1, device_id=peer, device_id_type=MESH)

    for copy in smalls:
        copy.wait()

    def lambda_list(slot):
        window = win * run + window_of(slot)
        if two_ends and slot == 1:
            low = jnp.where(window == 0, 0, window - 1)
            return [lambdas[low], lambdas[low + 1]]
        return [
            lambdas[jnp.maximum(window - 1, 0)],
            lambdas[window],
            lambdas[jnp.minimum(window + 1, windows - 1)],
        ]

    for copy in loads:
        copy.wait()

    pl.semaphore_wait(barrier, len(peers))

    counts = [0] * run

    def share_of(slot, owner):
        return bufs[slot].at[pl.ds(owner * own, own)]

    def descriptor(slot, owner, target, number):
        return pltpu.make_async_remote_copy(
            src_ref=share_of(slot, owner),
            dst_ref=share_of(slot, owner),
            send_sem=send_sem.at[slot, number],
            recv_sem=recv_sem.at[slot, owner],
            device_id={"grp": target},
            device_id_type=MESH,
        )

    sent = []

    def send(slot, owner, target):
        copy = descriptor(slot, owner, target, counts[slot])
        counts[slot] += 1
        copy.start()
        sent.append(copy)

    def arrived(slot, owner):
        descriptor(slot, owner, owner, 0).wait_recv()

    def to_x(slot, owner):
        for dx in range(1, dim_x):
            send(slot, owner, group_at(my_z, 0, dx))

    def to_y(slot, owner):
        for dy in range(1, dim_y):
            send(slot, owner, group_at(my_z, dy, 0))

    def open_sends(slot):
        for plane in planes[1:]:
            send(slot, grp, group_at(plane, 0, 0))
        to_x(slot, grp)
        to_y(slot, grp)

    def pass_column(slot, step):
        owner = group_at(planes[step], 0, 0)
        arrived(slot, owner)
        to_x(slot, owner)
        to_y(slot, owner)

    def pass_plane(slot, step):
        for dx in range(1, dim_x):
            owner = group_at(planes[step], 0, dx)
            arrived(slot, owner)
            if step % 2 == 0:
                to_y(slot, owner)
        for dy in range(1, dim_y):
            owner = group_at(planes[step], dy, 0)
            arrived(slot, owner)
            if step % 2 == 1:
                to_x(slot, owner)

    def last_arrivals(slot):
        for step in range(dim_z):
            for dy in range(1, dim_y):
                for dx in range(1, dim_x):
                    arrived(slot, group_at(planes[step], dy, dx))

    def spread(slot):
        lams = lambda_list(slot)
        count = fields_of(slot)
        depth = stage[slot, 4]
        inverse_root = lax.rsqrt(depth)
        sixth = jnp.exp(jnp.log(depth) * (-1.0 / 6.0))
        values = [stage[slot, f] for f in range(4)]
        values += [depth * inverse_root, sixth / stage[slot, 5]]
        values += [inverse_root * (1.0 - 0.5 * lam) for lam in lams]
        for f, value in enumerate(values):
            for part, piece in enumerate(split3(value)):
                feats[pl.ds((part * count + f) * own_pad, own_pad), :] = piece
        for row in range(3 * count, 32):
            feats[pl.ds(row * own_pad, own_pad), :] = jnp.zeros((own_pad, TILE), jnp.float32)
        source = lax.broadcasted_iota(jnp.int32, (32, count * TILE), 0)
        target = lax.broadcasted_iota(jnp.int32, (32, count * TILE), 1) // TILE
        picks = jnp.zeros((32, count * TILE), jnp.float32)
        for part in range(3):
            picks = jnp.where(source == target + part * count, 1.0, picks)
        picks = picks.astype(jnp.bfloat16)

        def one(block, carry):
            lines = feats[pl.ds(block, 32, stride=own_pad), :].astype(jnp.bfloat16)
            wide = lax.dot_general(
                lines, picks, (((0,), (0,)), ((), ())), preferred_element_type=jnp.float32
            )
            for f in range(count):
                for piece in range(PIECES):
                    rowbs[slot][(block * count + f) * PIECES + piece] = wide[
                        piece * ROWS : (piece + 1) * ROWS, f * TILE : (f + 1) * TILE
                    ]
            return carry

        lax.fori_loop(0, own, one, 0)

    def start_state(slot):
        zero = jnp.zeros((ROWS, TILE), jnp.float32)
        row = jnp.zeros((1, TILE), jnp.float32)
        return tuple(zero for _ in range(lams_of(slot))) + (row, row)

    def tiles(slot, first, last, state):
        local = window_of(slot)
        lams = lambda_list(slot)
        softs = [2.0 - lam for lam in lams]
        base = grp * own
        count = fields_of(slot)
        unroll = UNROLL if listed % UNROLL == 0 else 1

        def pair_sum(pair, state):
            row_id = row_ids[local, pair]
            col_id = col_ids[local, pair]
            col = [bufs[slot][col_id, f] for f in range(FIELDS)]
            mine = jnp.clip(row_id - base, 0, own - 1) * (count * PIECES)
            fields = [jnp.broadcast_to(col[f], (ROWS, TILE)) for f in range(3)]
            charge_col = col[3]
            depth_col = col[4]
            size_col = jnp.broadcast_to(1.0 / col[5], (ROWS, TILE))
            sum_disp = [None] * len(lams)
            sum_coul = [None] * len(lams)
            for piece in range(PIECES):
                wide = [rowbs[slot][mine + (f * PIECES + piece)] for f in range(count)]
                dx = wide[0] - fields[0]
                dy = wide[1] - fields[1]
                dz = wide[2] - fields[2]
                r2 = dx * dx + dy * dy + dz * dz
                scaled = r2 * (wide[5] * size_col)
                cube = scaled * scaled * scaled
                for k in range(len(lams)):
                    inverse = 1.0 / (cube + wide[FIELDS + k])
                    disp = inverse * (inverse - wide[4])
                    coul = wide[3] * lax.rsqrt(r2 + softs[k])
                    if piece == 0:
                        sum_disp[k], sum_coul[k] = disp, coul
                    else:
                        sum_disp[k] = sum_disp[k] + disp
                        sum_coul[k] = sum_coul[k] + coul
            depth_four = 4.0 * depth_col
            totals = [
                state[k] + (sum_disp[k] * depth_four + sum_coul[k] * charge_col)
                for k in range(len(lams))
            ]
            same = jnp.where(row_id == col_id, 1.0, 0.0)
            return tuple(totals) + (
                state[-2] + same * (depth_col * depth_col),
                state[-1] + same * (charge_col * charge_col),
            )

        def some(step, state):
            for part in range(unroll):
                state = pair_sum(step * unroll + part, state)
            return state

        return lax.fori_loop(first // unroll, last // unroll, some, state)

    def close(slot, state):
        sums = []
        for k, lam in enumerate(lambda_list(slot)):
            core = jnp.full((1, TILE), 1.0 - 0.5 * lam, jnp.float32)
            soft = jnp.full((1, TILE), 2.0 - lam, jnp.float32)
            inverse = 1.0 / core
            own_pairs = state[-2] * (4.0 * inverse * (inverse - 1.0)) + state[-1] * lax.rsqrt(soft)
            line = jnp.sum(state[k], axis=0, keepdims=True) - own_pairs
            sums.append(jnp.sum(line, axis=1, keepdims=True) * lam)
        if two_ends and slot == 1:
            sums = [sums[0], jnp.where(win == 0, sums[0], sums[1]), sums[1]]
        return sums

    for slot in range(run):
        open_sends(slot)
    for slot in range(run):
        spread(slot)

    shares = []
    lowers = []
    for wl in range(run):
        window = win * run + wl
        odd = (window + parity[0]) & 1
        lower = window - odd
        threshold = thresholds[0]
        for v in range(1, windows):
            threshold = jnp.where(lower == v, thresholds[v], threshold)
        drawn = ((threshold + parity[0]) & 1073741823) + 1
        share = jnp.full((ROWS, TILE), drawn, jnp.int32).astype(jnp.float32) * (1.0 / 1073741824.0)
        shares.append(-jnp.log(share))
        lowers.append(lower)

    for step in range(1, dim_z):
        pass_column(0, step)
        if step == 1:
            pass_plane(0, 0)
    for step in range(1, dim_z):
        pass_plane(0, step)
    if dim_z == 1:
        pass_plane(0, 0)
    if run > 1:
        for step in range(1, dim_z):
            pass_column(1, step)
    last_arrivals(0)
    for partner in partners:
        pl.semaphore_signal(ready, inc=1, device_id=partner, device_id_type=MESH)

    partial = []
    for slot in range(run):
        state = start_state(slot)
        first = 0
        if slot + 1 < run:
            if slot > 0:
                for step in range(1, dim_z):
                    pass_column(slot + 1, step)
            for step in range(dim_z):
                until = listed * (step + 1) // (2 * dim_z) // UNROLL * UNROLL
                state = tiles(slot, first, until, state)
                first = until
                pass_plane(slot + 1, step)
        state = tiles(slot, first, listed, state)
        if slot + 1 < run:
            last_arrivals(slot + 1)
        partial.append(close(slot, state))

    lane = lax.broadcasted_iota(jnp.int32, (1, TILE), 1)
    line = jnp.zeros((1, TILE), jnp.float32)
    for slot in range(run):
        place = (win * run + window_of(slot)) * 3
        for k in range(3):
            line = jnp.where(lane == place + k, partial[slot][k], line)
    red[me] = line
    for _ in partners:
        pl.semaphore_wait(ready, 1)
    everyone = wins * groups
    for other_win in range(wins):
        for step in range(groups):
            if other_win or step:
                target = ((win + other_win) % wins, (grp + step) % groups)
                pltpu.make_async_remote_copy(
                    src_ref=red.at[me],
                    dst_ref=red.at[me],
                    send_sem=red_send.at[0],
                    recv_sem=red_recv.at[0],
                    device_id=target,
                    device_id_type=MESH,
                ).start()
    for copy in sent:
        copy.wait_send()
    rest = pltpu.make_async_remote_copy(
        src_ref=red.at[pl.ds(0, everyone - 1)],
        dst_ref=red.at[pl.ds(0, everyone - 1)],
        send_sem=red_send.at[0],
        recv_sem=red_recv.at[0],
        device_id=((win + 1) % wins, (grp + 1) % groups),
        device_id_type=MESH,
    )
    rest.wait_recv()
    rest.wait_send()
    scale = 1.0 / (listed * groups * TILE * TILE)
    total = jnp.sum(red[0:everyone], axis=0) * scale
    energy = [
        [jnp.sum(jnp.where(lane == v * 3 + k, total, 0.0)) for k in range(3)]
        for v in range(windows)
    ]
    ups = [e[2] - e[1] for e in energy]
    downs = [e[0] - e[1] for e in energy]
    rows = lax.broadcasted_iota(jnp.int32, (ROWS, TILE), 0)
    lanes = lax.broadcasted_iota(jnp.int32, (ROWS, TILE), 1)
    cell = rows * TILE + lanes
    result = jnp.zeros((ROWS, TILE), jnp.float32)
    for wl in range(run):
        window = win * run + wl
        for k in range(3):
            value = energy[wl][k]
            for part in range(1, wins):
                value = jnp.where(win == part, energy[part * run + wl][k], value)
            result = jnp.where(cell == wl * TILE + k, value, result)
        profile = jnp.float32(0.0)
        change = jnp.float32(0.0)
        for v in range(windows):
            profile = profile + jnp.where(v < window, ups[v], 0.0)
            change = change + jnp.where(lowers[wl] == v, ups[v], 0.0)
            change = change + jnp.where(lowers[wl] + 1 == v, downs[v], 0.0)
        result = jnp.where(cell == (run + 1) * TILE + wl, profile, result)
        partner = jnp.logical_and(lowers[wl] >= 0, lowers[wl] + 1 < windows)
        margin = shares[wl] - inverse_temp[0] * change
        margin = jnp.where(partner, margin, 0.0)
        result = jnp.where(cell == run * TILE + wl, margin, result)
    out[...] = result


def finish(run, total, out_energy, out_margin, out_profile):
    out_energy[...] = total[0:run, 0:3]
    out_margin[...] = total[run, 0:run]
    out_profile[...] = total[run + 1, 0:run]


def per_device(dims, atom_table, row_blocks, col_blocks, lambdas, inverse_temp, parity, thresholds):
    run, fields, atoms = atom_table.shape
    wins = lax.axis_size("win")
    groups = lax.axis_size("grp")
    own = atoms // TILE
    listed = row_blocks.shape[1]
    cfg = (run, wins, groups, own, listed, dims)
    hbm = pl.BlockSpec(memory_space=pltpu.HBM)
    vmem = pl.BlockSpec(memory_space=pltpu.VMEM)
    smem = pl.BlockSpec(memory_space=pltpu.SMEM)
    own_pad = -(-own // 8) * 8
    counts = [9] * run
    if wins == 2 and run == 2:
        counts[1] = 8
    scratch = [pltpu.VMEM((groups * own, FIELDS, 1, TILE), jnp.float32) for _ in range(run)]
    scratch += [pltpu.VMEM((own * count * PIECES, ROWS, TILE), jnp.float32) for count in counts]
    scratch += [
        pltpu.VMEM((run, FIELDS, own_pad, TILE), jnp.float32),
        pltpu.VMEM((32 * own_pad, TILE), jnp.float32),
        pltpu.VMEM((wins * groups, 1, TILE), jnp.float32),
        pltpu.SMEM((run, listed), jnp.int32),
        pltpu.SMEM((run, listed), jnp.int32),
        pltpu.SMEM((wins * run,), jnp.float32),
        pltpu.SMEM((wins * run,), jnp.int32),
        pltpu.SemaphoreType.DMA((2 * run,)),
        pltpu.SemaphoreType.DMA((4,)),
        pltpu.SemaphoreType.DMA((run, max(1, messages_of(dims)))),
        pltpu.SemaphoreType.DMA((run, groups)),
        pltpu.SemaphoreType.DMA((1,)),
        pltpu.SemaphoreType.DMA((1,)),
        pltpu.SemaphoreType.REGULAR,
    ]
    table = jnp.transpose(atom_table.reshape(run, fields, own, TILE), (1, 2, 0, 3))
    total = pl.pallas_call(
        functools.partial(kernel, cfg),
        out_shape=jax.ShapeDtypeStruct((8, TILE), jnp.float32),
        in_specs=[hbm, hbm, hbm, hbm, smem, smem, hbm],
        out_specs=vmem,
        scratch_shapes=scratch,
        compiler_params=pltpu.CompilerParams(
            collective_id=0, has_side_effects=True, vmem_limit_bytes=LIMIT
        ),
    )(table, row_blocks, col_blocks, lambdas, inverse_temp, parity, thresholds)
    shapes = (
        jax.ShapeDtypeStruct((run, 3), jnp.float32),
        jax.ShapeDtypeStruct((run,), jnp.float32),
        jax.ShapeDtypeStruct((run,), jnp.float32),
    )
    return pl.pallas_call(
        functools.partial(finish, run),
        out_shape=shapes,
        in_specs=[vmem],
        out_specs=(vmem, vmem, vmem),
        compiler_params=pltpu.CompilerParams(vmem_limit_bytes=1024 * 1024),
    )(total)


def solution(mesh):
    return jax.shard_map(
        functools.partial(per_device, grid_of(mesh)),
        mesh=mesh,
        in_specs=(P("win", None, "grp"), P("win", "grp"), P("win", "grp"), P(), P(), P(), P()),
        out_specs=(P("win", None), P("win"), P("win")),
        check_vma=False,
    )
```

time: 45.8 us -> 39.8 us (0.87)
  Pallas kernels: 41.1 us -> 36 us
  local copies, waits for them, and re-layouts: 2.53 us -> 1.54 us
    pallas_call x1 -> x2, Pallas kernels: 41.1 us -> 36 us  [the longest x1 35.4 us: per_device(): pl.pallas_call(functools.partial(kernel, cfg), out_shape=jax.ShapeDtypeSt...]
    unnamed x12 -> x10, local copies, waits for them, and re-layouts: 2.53 us -> 1.54 us
where the time goes in v1:
time: 39.8 us; the launch traced here: 39.6 us
  Pallas kernels  36 us (90%)
  between operations  2 us (5%)
  local copies, waits for them, and re-layouts  1.54 us (4%)
    pallas_call x1, Pallas kernels, per_device(): pl.pallas_call(functools.partial(kernel, cfg), out_shape=jax.ShapeDtypeSt...  35.4 us
    unnamed x10, local copies, waits for them, and re-layouts  1.54 us

profile of v1, /device:TPU:0, one launch (start us, length us, event | category | flops | bytes accessed | tf_op | source)
XLA Modules:
  0.0 39.6 jit_solution(7627604186345773787)
XLA Ops:
  1.3 0.0 copy-start.2
  1.3 0.0 copy-start.4
  2.0 0.0 copy-start.1
  2.0 0.0 copy-start.3
  2.0 0.0 copy-done.2
  2.0 0.0 copy-done.4
  2.0 0.6 %copy-done.1 = s32[2,64]{1,0:T(2,128)S(1)} copy-done((s32[2,64]{1,0:T(2,128)S(1)}, s32[2,64]{1,0:T(2,128)}, u32[]{:S(2)}) %copy-start.1) | copy-done | bytes 536
  2.6 0.0 copy-done.3
  2.6 0.0 copy-start
  2.6 0.9 %copy-done = f32[2,6,1536]{2,0,1:T(2,128)S(1)} copy-done((f32[2,6,1536]{2,0,1:T(2,128)S(1)}, f32[2,6,1536]{2,0,1:T(2,128)}, u32[]{:S(2)}) %copy-start) | copy-done | bytes 73752
  3.5 35.4 %shard_map.94.total = f32[8,128]{1,0:T(8,128)S(1)} custom-call(f32[6,12,2,128]{3,2,1,0:T(2,128)S(1)} %bitcast.3, s32[2,64]{1,0:T(2,128)S(1)} %copy-done.1, s32[2,64]{1,0:T(2,128)S(1)} %copy-done.2, f32[4]{0:T(128)S(1)} %copy-done.3, f32[1]{0:T(128)S(6)} %copy.10.inverse_temp, s32[1]{0:T(128)S(6)} %copy.11.parity, s32[4]{0:T(128)S(1)} %copy-done.4), custom_call_target="tpu_custom_call" | custom-call | tf_op jit(solution)/shard_map/pallas_call | solution.py:510
  39.0 0.6 %shard_map.95 = (f32[2,3]{1,0:T(2,128)}, f32[2]{0:T(128)}, f32[2]{0:T(128)}) custom-call(f32[8,128]{1,0:T(8,128)S(1)} %shard_map.94.total), custom_call_target="tpu_custom_call" | custom-call | tf_op jit(solution)/shard_map/pallas_call | solution.py:525
Async XLA Ops:
  1.3 0.7 %copy-start.2 = (s32[2,64]{1,0:T(2,128)S(1)}, s32[2,64]{1,0:T(2,128)}, u32[]{:S(2)}) copy-start(s32[2,64]{1,0:T(2,128)} %col_hbm.1) | copy-start | bytes 1540
  1.3 0.7 %copy-start.4 = (s32[4]{0:T(128)S(1)}, s32[4]{0:T(128)}, u32[]{:S(2)}) copy-start(s32[4]{0:T(128)} %thresholds_hbm.1) | copy-start | bytes 52
  2.0 0.7 %copy-start.1 = (s32[2,64]{1,0:T(2,128)S(1)}, s32[2,64]{1,0:T(2,128)}, u32[]{:S(2)}) copy-start(s32[2,64]{1,0:T(2,128)} %row_hbm.1) | copy-start | bytes 1540
  2.0 0.7 %copy-start.3 = (f32[4]{0:T(128)S(1)}, f32[4]{0:T(128)}, u32[]{:S(2)}) copy-start(f32[4]{0:T(128)} %lambdas_hbm.1) | copy-start | bytes 52
  2.6 0.9 %copy-start = (f32[2,6,1536]{2,0,1:T(2,128)S(1)}, f32[2,6,1536]{2,0,1:T(2,128)}, u32[]{:S(2)}) copy-start(f32[2,6,1536]{2,0,1:T(2,128)} %param.7) | copy-start | bytes 221188

commit v2 on v1

--- a/solution.py
+++ b/solution.py
@@ -12,7 +12,10 @@
 FIELDS = 6
 PIECES = TILE // ROWS
 UNROLL = 4
-LIMIT = 48 * 1024 * 1024
+SPREAD = 4
+DIRECT = {(0, 0), (0, 1), (0, 2), (0, 3), (1, 2), (1, 3)}
+LINES = 40
+LIMIT = 67043328
 MESH = pl.DeviceIdType.MESH
 
 
@@ -38,10 +41,24 @@
 
 def messages_of(dims):
     z, y, x = dims
-    first = (z - 1) + (x - 1) + (y - 1)
-    second = (z - 1) * (x + y - 2)
-    third = z * (x - 1) * (y - 1)
-    return first + second + third
+    return (z - 1) + z * (x * y - 1)
+
+
+def near_steps(dims):
+    return min(2, dims[0])
+
+
+def phases_of(dims, groups, listed):
+    z, y, x = dims
+    slots = listed // groups + 1
+    ends = []
+    for step in range(near_steps(dims), z + 1):
+        ends.append(max(0, listed - slots * (z - step) * y * x))
+    return ends
+
+
+def bits_for(count):
+    return max(1, (count - 1).bit_length())
 
 
 def split3(value):
@@ -64,14 +81,20 @@
     *scratch,
 ):
     run, wins, groups, own, listed, dims = cfg
-    bufs = scratch[:run]
-    rowbs = scratch[run : 2 * run]
+    dim_z, dim_y, dim_x = dims
+    near = near_steps(dims)
+    parts = dim_z - near + 1
+    bufs = [scratch[slot * parts : (slot + 1) * parts] for slot in range(run)]
+    scratch = scratch[run * parts :]
+    rowbs = scratch[:run]
     (
         stage,
         feats,
         red,
         row_ids,
         col_ids,
+        words,
+        order,
         lambdas,
         thresholds,
         load_sem,
@@ -81,8 +104,8 @@
         red_send,
         red_recv,
         ready,
-    ) = scratch[2 * run :]
-    dim_z, dim_y, dim_x = dims
+        order_sem,
+    ) = scratch[run:]
     windows = wins * run
     win = lax.axis_index("win")
     grp = lax.axis_index("grp")
@@ -104,20 +127,39 @@
     def fields_of(slot):
         return FIELDS + lams_of(slot)
 
+    plane = dim_y * dim_x
+    span = plane * own
+    row_bits = bits_for(own)
+    index_bits = bits_for(near * span)
+
     def group_at(z, dy, dx):
         return (z * dim_y + (my_y + dy) % dim_y) * dim_x + (my_x + dx) % dim_x
 
-    def plane_at(step):
-        places = [
-            sorted(range(dim_z), key=lambda z: (abs(z - mine), z))[step]
-            for mine in range(dim_z)
-        ]
-        chosen = places[0]
-        for mine in range(1, dim_z):
-            chosen = jnp.where(my_z == mine, places[mine], chosen)
-        return chosen
-
-    planes = [my_z] + [plane_at(step) for step in range(1, dim_z)]
+    def place_at(dy, dx):
+        return ((my_y + dy) % dim_y) * dim_x + (my_x + dx) % dim_x
+
+    paired = dim_z & (dim_z - 1) == 0
+
+    def flipped(step):
+        other = 0
+        for bit in range(bits_for(dim_z)):
+            mine = (my_z // 2**bit) % 2
+            other = other + 2**bit * ((1 - mine) if (step >> bit) & 1 else mine)
+        return other
+
+    def plane_to(step):
+        return flipped(step) if paired else (my_z + step) % dim_z
+
+    def plane_from(step):
+        return flipped(step) if paired else (my_z - step + dim_z) % dim_z
+
+    def share_of(slot, step, place):
+        if step < near:
+            return bufs[slot][0].at[pl.ds((step * plane + place) * own, own)]
+        return bufs[slot][step - near + 1].at[pl.ds(place * own, own)]
+
+    my_place = place_at(0, 0)
+    others = [(dy, dx) for dy in range(dim_y) for dx in range(dim_x) if dy or dx]
 
     loads = []
     for slot in range(run):
@@ -126,7 +168,7 @@
             loads.append(
                 pltpu.make_async_copy(
                     table.at[f, :, local, :],
-                    bufs[slot].at[pl.ds(grp * own, own), f, 0, :],
+                    bufs[slot][0].at[pl.ds(my_place * own, own), f, 0, :],
                     load_sem.at[slot],
                 )
             )
@@ -152,9 +194,8 @@
 
     barrier = pltpu.get_barrier_semaphore()
     partners = [((win + step) % wins, grp) for step in range(1, wins)]
-    peers = [(win, group_at(plane, 0, 0)) for plane in planes[1:]]
-    peers += [(win, group_at(my_z, 0, dx)) for dx in range(1, dim_x)]
-    peers += [(win, group_at(my_z, dy, 0)) for dy in range(1, dim_y)]
+    peers = [(win, group_at(plane_to(step), 0, 0)) for step in range(1, dim_z)]
+    peers += [(win, group_at(my_z, dy, dx)) for dy, dx in others]
     peers += partners
     for peer in peers:
         pl.semaphore_signal(barrier, inc=1, device_id=peer, device_id_type=MESH)
@@ -173,74 +214,95 @@
             lambdas[jnp.minimum(window + 1, windows - 1)],
         ]
 
+    def sort_pairs(slot):
+        local = window_of(slot)
+        rows = row_ids[pl.ds(local, 1), :]
+        cols = col_ids[pl.ds(local, 1), :]
+        zone = jnp.zeros((1, listed), jnp.int32)
+        for z in range(1, dim_z):
+            zone = zone + jnp.where(cols >= z * span, 1, 0)
+        step_of = jnp.zeros((1, listed), jnp.int32)
+        for step in range(1, dim_z):
+            step_of = jnp.where(zone == plane_from(step), step, step_of)
+        index = cols - zone * span
+        index = index + jnp.where(step_of < near, step_of, 0) * span
+        mine = jnp.clip(rows - grp * own, 0, own - 1)
+        word = (step_of * 2**index_bits + index) * 2**row_bits + mine
+        word = word * 2 + jnp.where(rows == cols, 1, 0)
+        lane = lax.broadcasted_iota(jnp.int32, (listed, listed), 1)
+        line = lax.broadcasted_iota(jnp.int32, (listed, listed), 0)
+        eye = lane == line
+        rank = step_of * listed + lax.broadcasted_iota(jnp.int32, (1, listed), 1)
+        rank_row = jnp.broadcast_to(rank.astype(jnp.float32), (listed, listed))
+        word_row = jnp.broadcast_to(word.astype(jnp.float32), (listed, listed))
+        rank_col = jnp.sum(jnp.where(eye, rank_row, 0.0), axis=1, keepdims=True)
+        word_col = jnp.sum(jnp.where(eye, word_row, 0.0), axis=1, keepdims=True)
+        spot = jnp.sum(jnp.where(rank_row < rank_col, 1.0, 0.0), axis=1, keepdims=True)
+        hit = spot == lane.astype(jnp.float32)
+        sorted_row = jnp.sum(jnp.where(hit, word_col, 0.0), axis=0, keepdims=True)
+        words[pl.ds(slot, 1), :] = sorted_row.astype(jnp.int32)
+
     for copy in loads:
         copy.wait()
 
     pl.semaphore_wait(barrier, len(peers))
 
     counts = [0] * run
-
-    def share_of(slot, owner):
-        return bufs[slot].at[pl.ds(owner * own, own)]
-
-    def descriptor(slot, owner, target, number):
+    sent = []
+
+    def descriptor(slot, source, target_at, peer, number):
         return pltpu.make_async_remote_copy(
-            src_ref=share_of(slot, owner),
-            dst_ref=share_of(slot, owner),
+            src_ref=share_of(slot, *source),
+            dst_ref=share_of(slot, *target_at),
             send_sem=send_sem.at[slot, number],
-            recv_sem=recv_sem.at[slot, owner],
-            device_id={"grp": target},
+            recv_sem=recv_sem.at[slot, target_at[0], target_at[1]],
+            device_id={"grp": peer},
             device_id_type=MESH,
         )
 
-    sent = []
-
-    def send(slot, owner, target):
-        copy = descriptor(slot, owner, target, counts[slot])
+    def send(slot, source, target_at, peer):
+        copy = descriptor(slot, source, target_at, peer, counts[slot])
         counts[slot] += 1
         copy.start()
         sent.append(copy)
 
-    def arrived(slot, owner):
-        descriptor(slot, owner, owner, 0).wait_recv()
-
-    def to_x(slot, owner):
-        for dx in range(1, dim_x):
-            send(slot, owner, group_at(my_z, 0, dx))
-
-    def to_y(slot, owner):
-        for dy in range(1, dim_y):
-            send(slot, owner, group_at(my_z, dy, 0))
+    def arrived(slot, step, place):
+        at = (step, place)
+        descriptor(slot, at, at, grp, 0).wait_recv()
+
+    def to_plane(slot, step, place, dy, dx):
+        send(slot, (step, place), (step, place), group_at(my_z, dy, dx))
+
+    def to_direct(slot, step):
+        for dy, dx in others:
+            if (slot, step) in DIRECT or dy == 0 or dx == 0:
+                to_plane(slot, step, my_place, dy, dx)
 
     def open_sends(slot):
-        for plane in planes[1:]:
-            send(slot, grp, group_at(plane, 0, 0))
-        to_x(slot, grp)
-        to_y(slot, grp)
+        for step in range(1, dim_z):
+            send(slot, (0, my_place), (step, my_place), group_at(plane_to(step), 0, 0))
+        to_direct(slot, 0)
 
     def pass_column(slot, step):
-        owner = group_at(planes[step], 0, 0)
-        arrived(slot, owner)
-        to_x(slot, owner)
-        to_y(slot, owner)
+        arrived(slot, step, my_place)
+        to_direct(slot, step)
 
     def pass_plane(slot, step):
         for dx in range(1, dim_x):
-            owner = group_at(planes[step], 0, dx)
-            arrived(slot, owner)
-            if step % 2 == 0:
-                to_y(slot, owner)
+            arrived(slot, step, place_at(0, dx))
+            if (slot, step) not in DIRECT and step % 2 == 0:
+                for dy in range(1, dim_y):
+                    to_plane(slot, step, place_at(0, dx), dy, 0)
         for dy in range(1, dim_y):
-            owner = group_at(planes[step], dy, 0)
-            arrived(slot, owner)
-            if step % 2 == 1:
-                to_x(slot, owner)
-
-    def last_arrivals(slot):
-        for step in range(dim_z):
-            for dy in range(1, dim_y):
+            arrived(slot, step, place_at(dy, 0))
+            if (slot, step) not in DIRECT and step % 2 == 1:
                 for dx in range(1, dim_x):
-                    arrived(slot, group_at(planes[step], dy, dx))
+                    to_plane(slot, step, place_at(dy, 0), 0, dx)
+
+    def last_arrivals(slot, step):
+        for dy in range(1, dim_y):
+            for dx in range(1, dim_x):
+                arrived(slot, step, place_at(dy, dx))
 
     def spread(slot):
         lams = lambda_list(slot)
@@ -253,9 +315,9 @@
         values += [inverse_root * (1.0 - 0.5 * lam) for lam in lams]
         for f, value in enumerate(values):
             for part, piece in enumerate(split3(value)):
-                feats[pl.ds((part * count + f) * own_pad, own_pad), :] = piece
+                feats[pl.ds(part * count + f, own_pad, stride=LINES), :] = piece
         for row in range(3 * count, 32):
-            feats[pl.ds(row * own_pad, own_pad), :] = jnp.zeros((own_pad, TILE), jnp.float32)
+            feats[pl.ds(row, own_pad, stride=LINES), :] = jnp.zeros((own_pad, TILE), jnp.float32)
         source = lax.broadcasted_iota(jnp.int32, (32, count * TILE), 0)
         target = lax.broadcasted_iota(jnp.int32, (32, count * TILE), 1) // TILE
         picks = jnp.zeros((32, count * TILE), jnp.float32)
@@ -263,8 +325,9 @@
             picks = jnp.where(source == target + part * count, 1.0, picks)
         picks = picks.astype(jnp.bfloat16)
 
-        def one(block, carry):
-            lines = feats[pl.ds(block, 32, stride=own_pad), :].astype(jnp.bfloat16)
+        def one(block):
+            start = pl.multiple_of(block * LINES, 8)
+            lines = feats[pl.ds(start, 32), :].astype(jnp.bfloat16)
             wide = lax.dot_general(
                 lines, picks, (((0,), (0,)), ((), ())), preferred_element_type=jnp.float32
             )
@@ -273,28 +336,40 @@
                     rowbs[slot][(block * count + f) * PIECES + piece] = wide[
                         piece * ROWS : (piece + 1) * ROWS, f * TILE : (f + 1) * TILE
                     ]
+
+        def some(step, carry):
+            for part in range(together):
+                one(step * together + part)
             return carry
 
-        lax.fori_loop(0, own, one, 0)
+        together = SPREAD if own % SPREAD == 0 else 1
+        lax.fori_loop(0, own // together, some, 0)
 
     def start_state(slot):
         zero = jnp.zeros((ROWS, TILE), jnp.float32)
         row = jnp.zeros((1, TILE), jnp.float32)
         return tuple(zero for _ in range(lams_of(slot))) + (row, row)
 
-    def tiles(slot, first, last, state):
-        local = window_of(slot)
+    def tiles(slot, phase, first, last, state):
         lams = lambda_list(slot)
         softs = [2.0 - lam for lam in lams]
-        base = grp * own
         count = fields_of(slot)
-        unroll = UNROLL if listed % UNROLL == 0 else 1
+        unroll = max(u for u in (1, 2, UNROLL) if (last - first) % u == 0)
 
         def pair_sum(pair, state):
-            row_id = row_ids[local, pair]
-            col_id = col_ids[local, pair]
-            col = [bufs[slot][col_id, f] for f in range(FIELDS)]
-            mine = jnp.clip(row_id - base, 0, own - 1) * (count * PIECES)
+            word = order[slot, pair]
+            same = (word & 1).astype(jnp.float32)
+            mine = jnp.clip((word >> 1) & (2**row_bits - 1), 0, own - 1) * (count * PIECES)
+            index = jnp.clip((word >> (1 + row_bits)) & (2**index_bits - 1), 0, near * span - 1)
+            step_of = word >> (1 + row_bits + index_bits)
+            col = [bufs[slot][0][index, f] for f in range(FIELDS)]
+            if phase > 0:
+                far = jnp.clip(jnp.where(step_of < near, 0, index), 0, span - 1)
+                for part in range(1, phase + 1):
+                    here = step_of == near + part - 1
+                    col = [
+                        jnp.where(here, bufs[slot][part][far, f], col[f]) for f in range(FIELDS)
+                    ]
             fields = [jnp.broadcast_to(col[f], (ROWS, TILE)) for f in range(3)]
             charge_col = col[3]
             depth_col = col[4]
@@ -323,7 +398,6 @@
                 state[k] + (sum_disp[k] * depth_four + sum_coul[k] * charge_col)
                 for k in range(len(lams))
             ]
-            same = jnp.where(row_id == col_id, 1.0, 0.0)
             return tuple(totals) + (
                 state[-2] + same * (depth_col * depth_col),
                 state[-1] + same * (charge_col * charge_col),
@@ -331,10 +405,10 @@
 
         def some(step, state):
             for part in range(unroll):
-                state = pair_sum(step * unroll + part, state)
+                state = pair_sum(first + step * unroll + part, state)
             return state
 
-        return lax.fori_loop(first // unroll, last // unroll, some, state)
+        return lax.fori_loop(0, (last - first) // unroll, some, state)
 
     def close(slot, state):
         sums = []
@@ -352,6 +426,15 @@
     for slot in range(run):
         open_sends(slot)
     for slot in range(run):
+        sort_pairs(slot)
+    ordered = pltpu.make_async_copy(words, order, order_sem)
+    ordered.start()
+    spread(0)
+    if dim_z > 1:
+        pass_column(0, 1)
+    if run > 1:
+        pass_plane(1, 0)
+    for slot in range(1, run):
         spread(slot)
 
     shares = []
@@ -368,37 +451,63 @@
         shares.append(-jnp.log(share))
         lowers.append(lower)
 
-    for step in range(1, dim_z):
+    if dim_z > 2:
+        pass_column(0, 2)
+    if run > 1 and dim_z > 1:
+        pass_column(1, 1)
+    for step in range(3, dim_z):
         pass_column(0, step)
-        if step == 1:
-            pass_plane(0, 0)
-    for step in range(1, dim_z):
-        pass_plane(0, step)
-    if dim_z == 1:
-        pass_plane(0, 0)
+    ordered.wait()
+    ends = phases_of(dims, groups, listed)
+
+    def complete(slot, phase):
+        steps = range(near) if phase == 0 else [near + phase - 1]
+        for step in steps:
+            if slot == 0:
+                pass_plane(slot, step)
+            last_arrivals(slot, step)
+
     if run > 1:
-        for step in range(1, dim_z):
-            pass_column(1, step)
-    last_arrivals(0)
-    for partner in partners:
-        pl.semaphore_signal(ready, inc=1, device_id=partner, device_id_type=MESH)
-
+        later = [functools.partial(pass_plane, 1, step) for step in range(1, min(2, dim_z))]
+        for step in range(2, dim_z):
+            later.append(functools.partial(pass_column, 1, step))
+        for step in range(2, dim_z):
+            later.append(functools.partial(pass_plane, 1, step))
+    else:
+        later = []
     partial = []
     for slot in range(run):
         state = start_state(slot)
         first = 0
-        if slot + 1 < run:
-            if slot > 0:
-                for step in range(1, dim_z):
-                    pass_column(slot + 1, step)
-            for step in range(dim_z):
-                until = listed * (step + 1) // (2 * dim_z) // UNROLL * UNROLL
-                state = tiles(slot, first, until, state)
-                first = until
-                pass_plane(slot + 1, step)
-        state = tiles(slot, first, listed, state)
-        if slot + 1 < run:
-            last_arrivals(slot + 1)
+        if slot > 1:
+            pass_plane(slot, 0)
+            for step in range(1, dim_z):
+                pass_column(slot, step)
+            for step in range(1, dim_z):
+                pass_plane(slot, step)
+        cuts = []
+        for phase, end in enumerate(ends):
+            if slot == 0 and (end - first) % 8 == 0:
+                cuts.append((phase, first, first + (end - first) // 2))
+                cuts.append((phase, first + (end - first) // 2, end))
+            else:
+                cuts.append((phase, first, end))
+            first = end
+        done = -1
+        for number, (phase, first, last) in enumerate(cuts):
+            if phase != done:
+                complete(slot, phase)
+                done = phase
+                if slot == 0 and phase == len(ends) - 1:
+                    for partner in partners:
+                        pl.semaphore_signal(ready, inc=1, device_id=partner, device_id_type=MESH)
+            if last > first:
+                state = tiles(slot, phase, first, last, state)
+            if slot == 0 and later:
+                later.pop(0)()
+                if number == len(cuts) - 1:
+                    while later:
+                        later.pop(0)()
         partial.append(close(slot, state))
 
     lane = lax.broadcasted_iota(jnp.int32, (1, TILE), 1)
@@ -488,23 +597,31 @@
     counts = [9] * run
     if wins == 2 and run == 2:
         counts[1] = 8
-    scratch = [pltpu.VMEM((groups * own, FIELDS, 1, TILE), jnp.float32) for _ in range(run)]
+    near = near_steps(dims)
+    span = dims[1] * dims[2] * own
+    scratch = []
+    for _ in range(run):
+        for planes in [near] + [1] * (dims[0] - near):
+            scratch.append(pltpu.VMEM((planes * span, FIELDS, 1, TILE), jnp.float32))
     scratch += [pltpu.VMEM((own * count * PIECES, ROWS, TILE), jnp.float32) for count in counts]
     scratch += [
         pltpu.VMEM((run, FIELDS, own_pad, TILE), jnp.float32),
-        pltpu.VMEM((32 * own_pad, TILE), jnp.float32),
+        pltpu.VMEM((LINES * (own_pad + 1), TILE), jnp.float32),
         pltpu.VMEM((wins * groups, 1, TILE), jnp.float32),
-        pltpu.SMEM((run, listed), jnp.int32),
+        pltpu.VMEM((run, listed), jnp.int32),
+        pltpu.VMEM((run, listed), jnp.int32),
+        pltpu.VMEM((run, listed), jnp.int32),
         pltpu.SMEM((run, listed), jnp.int32),
         pltpu.SMEM((wins * run,), jnp.float32),
         pltpu.SMEM((wins * run,), jnp.int32),
         pltpu.SemaphoreType.DMA((2 * run,)),
         pltpu.SemaphoreType.DMA((4,)),
         pltpu.SemaphoreType.DMA((run, max(1, messages_of(dims)))),
-        pltpu.SemaphoreType.DMA((run, groups)),
+        pltpu.SemaphoreType.DMA((run, dims[0], dims[1] * dims[2])),
         pltpu.SemaphoreType.DMA((1,)),
         pltpu.SemaphoreType.DMA((1,)),
         pltpu.SemaphoreType.REGULAR,
+        pltpu.SemaphoreType.DMA,
     ]
     table = jnp.transpose(atom_table.reshape(run, fields, own, TILE), (1, 2, 0, 3))
     total = pl.pallas_call(

time: 39.8 us -> 35.5 us (0.89)
  Pallas kernels: 36 us -> 32.6 us
  local copies, waits for them, and re-layouts: 1.54 us -> 0.66 us
    pallas_call x1, Pallas kernels: 35.4 us -> 32.1 us  [per_device(): pl.pallas_call(functools.partial(kernel, cfg), out_shape=jax.ShapeDtypeSt...]
    unnamed x10 -> x2, local copies, waits for them, and re-layouts: 1.54 us -> 0.66 us
where the time goes in v2:
time: 35.5 us; the launch traced here: 35.2 us
  Pallas kernels  32.6 us (92%)
  between operations  1.94 us (5%)
  local copies, waits for them, and re-layouts  0.66 us (2%)
    pallas_call x1, Pallas kernels, per_device(): pl.pallas_call(functools.partial(kernel, cfg), out_shape=jax.ShapeDtypeSt...  32.1 us

profile of v2, /device:TPU:0, one launch (start us, length us, event | category | flops | bytes accessed | tf_op | source)
XLA Modules:
  0.0 35.2 jit_solution(11105496701231549242)
XLA Ops:
  1.9 32.1 %shard_map.94.total = f32[8,128]{1,0:T(8,128)} custom-call(f32[6,12,2,128]{3,2,1,0:T(2,128)} %bitcast.3, s32[2,64]{1,0:T(2,128)} %row_hbm.1, s32[2,64]{1,0:T(2,128)} %col_hbm.1, f32[4]{0:T(128)} %lambdas_hbm.1, f32[1]{0:T(128)S(6)} %copy.10.inverse_temp, s32[1]{0:T(128)S(6)} %copy.11.parity, s32[4]{0:T(128)} %thresholds_hbm.1), custom_call_target="tpu_custom_call" | custom-call | tf_op jit(solution)/shard_map/pallas_call | solution.py:627
  34.0 0.0 copy-start
  34.0 0.7 %copy-done = f32[8,128]{1,0:T(8,128)S(1)} copy-done((f32[8,128]{1,0:T(8,128)S(1)}, f32[8,128]{1,0:T(8,128)}, u32[]{:S(2)}) %copy-start) | copy-done | bytes 4120
  34.7 0.6 %shard_map.95 = (f32[2,3]{1,0:T(2,128)}, f32[2]{0:T(128)}, f32[2]{0:T(128)}) custom-call(f32[8,128]{1,0:T(8,128)S(1)} %copy-done), custom_call_target="tpu_custom_call" | custom-call | tf_op jit(solution)/shard_map/pallas_call | solution.py:642
Async XLA Ops:
  34.0 0.7 %copy-start = (f32[8,128]{1,0:T(8,128)S(1)}, f32[8,128]{1,0:T(8,128)}, u32[]{:S(2)}) copy-start(f32[8,128]{1,0:T(8,128)} %shard_map.94.total) | copy-start | bytes 12292

commit v3 on v2

--- a/solution.py
+++ b/solution.py
@@ -13,7 +13,6 @@
 PIECES = TILE // ROWS
 UNROLL = 4
 SPREAD = 4
-DIRECT = {(0, 0), (0, 1), (0, 2), (0, 3), (1, 2), (1, 3)}
 LINES = 40
 LIMIT = 67043328
 MESH = pl.DeviceIdType.MESH
@@ -48,9 +47,13 @@
     return min(2, dims[0])
 
 
+def slots_of(groups, listed):
+    return listed // groups + 1
+
+
 def phases_of(dims, groups, listed):
     z, y, x = dims
-    slots = listed // groups + 1
+    slots = slots_of(groups, listed)
     ends = []
     for step in range(near_steps(dims), z + 1):
         ends.append(max(0, listed - slots * (z - step) * y * x))
@@ -86,6 +89,8 @@
     parts = dim_z - near + 1
     bufs = [scratch[slot * parts : (slot + 1) * parts] for slot in range(run)]
     scratch = scratch[run * parts :]
+    zin = [scratch[slot * dim_z : (slot + 1) * dim_z] for slot in range(run)]
+    scratch = scratch[run * dim_z :]
     rowbs = scratch[:run]
     (
         stage,
@@ -95,6 +100,9 @@
         col_ids,
         words,
         order,
+        packs,
+        asks,
+        asked,
         lambdas,
         thresholds,
         load_sem,
@@ -105,6 +113,9 @@
         red_recv,
         ready,
         order_sem,
+        ask_send,
+        ask_recv,
+        asked_sem,
     ) = scratch[run:]
     windows = wins * run
     win = lax.axis_index("win")
@@ -130,7 +141,10 @@
     plane = dim_y * dim_x
     span = plane * own
     row_bits = bits_for(own)
-    index_bits = bits_for(near * span)
+    slots = slots_of(groups, listed)
+    unit = plane * slots
+    index_bits = bits_for(near * unit)
+    width = asks.shape[3]
 
     def group_at(z, dy, dx):
         return (z * dim_y + (my_y + dy) % dim_y) * dim_x + (my_x + dx) % dim_x
@@ -153,10 +167,14 @@
     def plane_from(step):
         return flipped(step) if paired else (my_z - step + dim_z) % dim_z
 
-    def share_of(slot, step, place):
+    def part_of(slot, step):
         if step < near:
-            return bufs[slot][0].at[pl.ds((step * plane + place) * own, own)]
-        return bufs[slot][step - near + 1].at[pl.ds(place * own, own)]
+            return bufs[slot][0], step * unit
+        return bufs[slot][step - near + 1], 0
+
+    def slots_at(slot, step, place):
+        ref, base = part_of(slot, step)
+        return ref.at[pl.ds(base + place * slots, slots)]
 
     my_place = place_at(0, 0)
     others = [(dy, dx) for dy in range(dim_y) for dx in range(dim_x) if dy or dx]
@@ -168,7 +186,7 @@
             loads.append(
                 pltpu.make_async_copy(
                     table.at[f, :, local, :],
-                    bufs[slot][0].at[pl.ds(my_place * own, own), f, 0, :],
+                    zin[slot][0].at[:, f, 0, :],
                     load_sem.at[slot],
                 )
             )
@@ -224,23 +242,49 @@
         step_of = jnp.zeros((1, listed), jnp.int32)
         for step in range(1, dim_z):
             step_of = jnp.where(zone == plane_from(step), step, step_of)
-        index = cols - zone * span
-        index = index + jnp.where(step_of < near, step_of, 0) * span
+        inside = cols - zone * span
+        place = jnp.zeros((1, listed), jnp.int32)
+        for spot in range(1, plane):
+            place = place + jnp.where(inside >= spot * own, 1, 0)
         mine = jnp.clip(rows - grp * own, 0, own - 1)
-        word = (step_of * 2**index_bits + index) * 2**row_bits + mine
-        word = word * 2 + jnp.where(rows == cols, 1, 0)
+        key = place * dim_z + step_of
+        packed = (key * 2**row_bits + (inside - place * own)) * 2**row_bits + mine
+        packed = packed * 2 + jnp.where(rows == cols, 1, 0)
         lane = lax.broadcasted_iota(jnp.int32, (listed, listed), 1)
         line = lax.broadcasted_iota(jnp.int32, (listed, listed), 0)
-        eye = lane == line
-        rank = step_of * listed + lax.broadcasted_iota(jnp.int32, (1, listed), 1)
-        rank_row = jnp.broadcast_to(rank.astype(jnp.float32), (listed, listed))
-        word_row = jnp.broadcast_to(word.astype(jnp.float32), (listed, listed))
-        rank_col = jnp.sum(jnp.where(eye, rank_row, 0.0), axis=1, keepdims=True)
-        word_col = jnp.sum(jnp.where(eye, word_row, 0.0), axis=1, keepdims=True)
-        spot = jnp.sum(jnp.where(rank_row < rank_col, 1.0, 0.0), axis=1, keepdims=True)
-        hit = spot == lane.astype(jnp.float32)
-        sorted_row = jnp.sum(jnp.where(hit, word_col, 0.0), axis=0, keepdims=True)
+        packed_row = jnp.broadcast_to(packed.astype(jnp.float32), (listed, listed))
+        packed_col = jnp.sum(jnp.where(lane == line, packed_row, 0.0), axis=1, keepdims=True)
+        packed_col = jnp.broadcast_to(packed_col.astype(jnp.int32), (listed, listed))
+        low = packed_col & (2 ** (row_bits + 1) - 1)
+        block = (packed_col >> (row_bits + 1)) & (2**row_bits - 1)
+        key_col = packed_col >> (2 * row_bits + 1)
+        key_row = jnp.broadcast_to(key, (listed, listed))
+        earlier = jnp.where(jnp.logical_and(key_row == key_col, lane < line), 1.0, 0.0)
+        count = jnp.sum(earlier, axis=1, keepdims=True).astype(jnp.int32)
+        count = jnp.minimum(jnp.broadcast_to(count, (listed, listed)), slots - 1)
+        step_col = key_col % dim_z
+        place_col = key_col // dim_z
+        rank_col = step_col * listed + line
+        rank_row = jnp.broadcast_to(step_of, (listed, listed)) * listed + lane
+        before = jnp.where(rank_row < rank_col, 1.0, 0.0)
+        target = jnp.sum(before, axis=1, keepdims=True).astype(jnp.int32)
+        index = place_col * slots + count
+        index = index + jnp.where(step_col < near, step_col, 0) * unit
+        word = (step_col * 2**index_bits + index) * 2 ** (row_bits + 1) + low
+        hit = jnp.broadcast_to(target, (listed, listed)) == lane
+        sorted_row = jnp.sum(jnp.where(hit, word.astype(jnp.float32), 0.0), axis=0, keepdims=True)
         words[pl.ds(slot, 1), :] = sorted_row.astype(jnp.int32)
+        wide_lane = lax.broadcasted_iota(jnp.int32, (listed, width), 1)
+        spots = (key_col * slots + count)[:, 0:1]
+        chosen = jnp.where(
+            jnp.broadcast_to(spots, (listed, width)) == wide_lane,
+            jnp.broadcast_to(block[:, 0:1], (listed, width)).astype(jnp.float32),
+            0.0,
+        )
+        asks[my_place, slot] = jnp.sum(chosen, axis=0, keepdims=True).astype(jnp.int32)
+
+    for slot in range(run):
+        sort_pairs(slot)
 
     for copy in loads:
         copy.wait()
@@ -250,59 +294,94 @@
     counts = [0] * run
     sent = []
 
-    def descriptor(slot, source, target_at, peer, number):
-        return pltpu.make_async_remote_copy(
-            src_ref=share_of(slot, *source),
-            dst_ref=share_of(slot, *target_at),
+    def begin(source, target, number, receive, peer, slot):
+        copy = pltpu.make_async_remote_copy(
+            src_ref=source,
+            dst_ref=target,
             send_sem=send_sem.at[slot, number],
-            recv_sem=recv_sem.at[slot, target_at[0], target_at[1]],
+            recv_sem=receive,
             device_id={"grp": peer},
             device_id_type=MESH,
         )
-
-    def send(slot, source, target_at, peer):
-        copy = descriptor(slot, source, target_at, peer, counts[slot])
+        return copy
+
+    def send(slot, source, target, receive, peer):
+        copy = begin(source, target, counts[slot], receive, peer, slot)
         counts[slot] += 1
         copy.start()
         sent.append(copy)
 
-    def arrived(slot, step, place):
-        at = (step, place)
-        descriptor(slot, at, at, grp, 0).wait_recv()
-
-    def to_plane(slot, step, place, dy, dx):
-        send(slot, (step, place), (step, place), group_at(my_z, dy, dx))
-
-    def to_direct(slot, step):
+    asking = []
+    for number, (dy, dx) in enumerate(others):
+        asking.append(
+            pltpu.make_async_remote_copy(
+                src_ref=asks.at[my_place],
+                dst_ref=asks.at[my_place],
+                send_sem=ask_send.at[number],
+                recv_sem=ask_recv.at[my_place],
+                device_id={"grp": group_at(my_z, dy, dx)},
+                device_id_type=MESH,
+            )
+        )
+    for copy in asking:
+        copy.start()
+
+    def questions():
         for dy, dx in others:
-            if (slot, step) in DIRECT or dy == 0 or dx == 0:
-                to_plane(slot, step, my_place, dy, dx)
+            place = place_at(dy, dx)
+            pltpu.make_async_remote_copy(
+                src_ref=asks.at[place],
+                dst_ref=asks.at[place],
+                send_sem=ask_send.at[0],
+                recv_sem=ask_recv.at[place],
+                device_id={"grp": group_at(my_z, dy, dx)},
+                device_id_type=MESH,
+            ).wait_recv()
+        copy = pltpu.make_async_copy(asks, asked, asked_sem)
+        copy.start()
+        return copy
 
     def open_sends(slot):
         for step in range(1, dim_z):
-            send(slot, (0, my_place), (step, my_place), group_at(plane_to(step), 0, 0))
-        to_direct(slot, 0)
-
-    def pass_column(slot, step):
-        arrived(slot, step, my_place)
-        to_direct(slot, step)
-
-    def pass_plane(slot, step):
-        for dx in range(1, dim_x):
-            arrived(slot, step, place_at(0, dx))
-            if (slot, step) not in DIRECT and step % 2 == 0:
-                for dy in range(1, dim_y):
-                    to_plane(slot, step, place_at(0, dx), dy, 0)
-        for dy in range(1, dim_y):
-            arrived(slot, step, place_at(dy, 0))
-            if (slot, step) not in DIRECT and step % 2 == 1:
-                for dx in range(1, dim_x):
-                    to_plane(slot, step, place_at(dy, 0), 0, dx)
-
-    def last_arrivals(slot, step):
-        for dy in range(1, dim_y):
-            for dx in range(1, dim_x):
-                arrived(slot, step, place_at(dy, dx))
+            peer = group_at(plane_to(step), 0, 0)
+            send(slot, zin[slot][0], zin[slot][step], recv_sem.at[slot, step, my_place], peer)
+
+    def answer(slot, step):
+        if step:
+            share = zin[slot][step]
+            begin(share, share, 0, recv_sem.at[slot, step, my_place], grp, slot).wait_recv()
+        share = zin[slot][step]
+
+        def named(place, part):
+            block = asked[place, slot, 0, (my_place * dim_z + step) * slots + part]
+            return jnp.clip(block, 0, own - 1)
+
+        for number, (dy, dx) in enumerate(others):
+            first = (step * len(others) + number) * slots
+            for part in range(slots):
+                block = named(place_at(dy, dx), part)
+                for f in range(FIELDS):
+                    packs[slot, first + part, f] = share[block, f]
+        for number, (dy, dx) in enumerate(others):
+            first = (step * len(others) + number) * slots
+            send(
+                slot,
+                packs.at[slot, pl.ds(first, slots)],
+                slots_at(slot, step, my_place),
+                recv_sem.at[slot, step, my_place],
+                group_at(my_z, dy, dx),
+            )
+        ref, base = part_of(slot, step)
+        for part in range(slots):
+            block = named(my_place, part)
+            for f in range(FIELDS):
+                ref[base + my_place * slots + part, f] = share[block, f]
+
+    def answered(slot, step):
+        for dy, dx in others:
+            place = place_at(dy, dx)
+            ref = slots_at(slot, step, place)
+            begin(ref, ref, 0, recv_sem.at[slot, step, place], grp, slot).wait_recv()
 
     def spread(slot):
         lams = lambda_list(slot)
@@ -360,11 +439,11 @@
             word = order[slot, pair]
             same = (word & 1).astype(jnp.float32)
             mine = jnp.clip((word >> 1) & (2**row_bits - 1), 0, own - 1) * (count * PIECES)
-            index = jnp.clip((word >> (1 + row_bits)) & (2**index_bits - 1), 0, near * span - 1)
+            index = jnp.clip((word >> (1 + row_bits)) & (2**index_bits - 1), 0, near * unit - 1)
             step_of = word >> (1 + row_bits + index_bits)
             col = [bufs[slot][0][index, f] for f in range(FIELDS)]
             if phase > 0:
-                far = jnp.clip(jnp.where(step_of < near, 0, index), 0, span - 1)
+                far = jnp.clip(jnp.where(step_of < near, 0, index), 0, unit - 1)
                 for part in range(1, phase + 1):
                     here = step_of == near + part - 1
                     col = [
@@ -425,15 +504,16 @@
 
     for slot in range(run):
         open_sends(slot)
-    for slot in range(run):
-        sort_pairs(slot)
     ordered = pltpu.make_async_copy(words, order, order_sem)
     ordered.start()
     spread(0)
+    known = questions()
+    known.wait()
+    answer(0, 0)
     if dim_z > 1:
-        pass_column(0, 1)
-    if run > 1:
-        pass_plane(1, 0)
+        answer(0, 1)
+    for slot in range(1, run):
+        answer(slot, 0)
     for slot in range(1, run):
         spread(slot)
 
@@ -451,63 +531,37 @@
         shares.append(-jnp.log(share))
         lowers.append(lower)
 
-    if dim_z > 2:
-        pass_column(0, 2)
-    if run > 1 and dim_z > 1:
-        pass_column(1, 1)
-    for step in range(3, dim_z):
-        pass_column(0, step)
+    for step in range(2, dim_z):
+        answer(0, step)
+        if run > 1:
+            answer(1, step - 1)
     ordered.wait()
     ends = phases_of(dims, groups, listed)
 
     def complete(slot, phase):
-        steps = range(near) if phase == 0 else [near + phase - 1]
-        for step in steps:
-            if slot == 0:
-                pass_plane(slot, step)
-            last_arrivals(slot, step)
-
-    if run > 1:
-        later = [functools.partial(pass_plane, 1, step) for step in range(1, min(2, dim_z))]
-        for step in range(2, dim_z):
-            later.append(functools.partial(pass_column, 1, step))
-        for step in range(2, dim_z):
-            later.append(functools.partial(pass_plane, 1, step))
-    else:
-        later = []
+        for step in range(near) if phase == 0 else [near + phase - 1]:
+            answered(slot, step)
+
+    later = []
+    for slot in range(1, run):
+        first_step = dim_z - 1 if slot == 1 and dim_z > 2 else 1
+        later += [functools.partial(answer, slot, step) for step in range(first_step, dim_z)]
     partial = []
     for slot in range(run):
         state = start_state(slot)
         first = 0
-        if slot > 1:
-            pass_plane(slot, 0)
-            for step in range(1, dim_z):
-                pass_column(slot, step)
-            for step in range(1, dim_z):
-                pass_plane(slot, step)
-        cuts = []
         for phase, end in enumerate(ends):
-            if slot == 0 and (end - first) % 8 == 0:
-                cuts.append((phase, first, first + (end - first) // 2))
-                cuts.append((phase, first + (end - first) // 2, end))
-            else:
-                cuts.append((phase, first, end))
+            complete(slot, phase)
+            if slot == 0 and phase == len(ends) - 1:
+                for partner in partners:
+                    pl.semaphore_signal(ready, inc=1, device_id=partner, device_id_type=MESH)
+            if end > first:
+                state = tiles(slot, phase, first, end, state)
             first = end
-        done = -1
-        for number, (phase, first, last) in enumerate(cuts):
-            if phase != done:
-                complete(slot, phase)
-                done = phase
-                if slot == 0 and phase == len(ends) - 1:
-                    for partner in partners:
-                        pl.semaphore_signal(ready, inc=1, device_id=partner, device_id_type=MESH)
-            if last > first:
-                state = tiles(slot, phase, first, last, state)
             if slot == 0 and later:
                 later.pop(0)()
-                if number == len(cuts) - 1:
-                    while later:
-                        later.pop(0)()
+        while later:
+            later.pop(0)()
         partial.append(close(slot, state))
 
     lane = lax.broadcasted_iota(jnp.int32, (1, TILE), 1)
@@ -532,7 +586,7 @@
                     device_id=target,
                     device_id_type=MESH,
                 ).start()
-    for copy in sent:
+    for copy in sent + asking:
         copy.wait_send()
     rest = pltpu.make_async_remote_copy(
         src_ref=red.at[pl.ds(0, everyone - 1)],
@@ -598,11 +652,16 @@
     if wins == 2 and run == 2:
         counts[1] = 8
     near = near_steps(dims)
-    span = dims[1] * dims[2] * own
+    plane = dims[1] * dims[2]
+    slots = slots_of(groups, listed)
+    unit = plane * slots
+    width = -(-plane * dims[0] * slots // TILE) * TILE
+    answers = max(1, dims[0] * (plane - 1) * slots)
     scratch = []
     for _ in range(run):
         for planes in [near] + [1] * (dims[0] - near):
-            scratch.append(pltpu.VMEM((planes * span, FIELDS, 1, TILE), jnp.float32))
+            scratch.append(pltpu.VMEM((planes * unit, FIELDS, 1, TILE), jnp.float32))
+    scratch += [pltpu.VMEM((own, FIELDS, 1, TILE), jnp.float32) for _ in range(run * dims[0])]
     scratch += [pltpu.VMEM((own * count * PIECES, ROWS, TILE), jnp.float32) for count in counts]
     scratch += [
         pltpu.VMEM((run, FIELDS, own_pad, TILE), jnp.float32),
@@ -612,6 +671,9 @@
         pltpu.VMEM((run, listed), jnp.int32),
         pltpu.VMEM((run, listed), jnp.int32),
         pltpu.SMEM((run, listed), jnp.int32),
+        pltpu.VMEM((run, answers, FIELDS, 1, TILE), jnp.float32),
+        pltpu.VMEM((plane, run, 1, width), jnp.int32),
+        pltpu.SMEM((plane, run, 1, width), jnp.int32),
         pltpu.SMEM((wins * run,), jnp.float32),
         pltpu.SMEM((wins * run,), jnp.int32),
         pltpu.SemaphoreType.DMA((2 * run,)),
@@ -621,6 +683,9 @@
         pltpu.SemaphoreType.DMA((1,)),
         pltpu.SemaphoreType.DMA((1,)),
         pltpu.SemaphoreType.REGULAR,
+        pltpu.SemaphoreType.DMA,
+        pltpu.SemaphoreType.DMA((plane,)),
+        pltpu.SemaphoreType.DMA((plane,)),
         pltpu.SemaphoreType.DMA,
     ]
     table = jnp.transpose(atom_table.reshape(run, fields, own, TILE), (1, 2, 0, 3))

time: 35.5 us -> 33.7 us (0.949)
  Pallas kernels: 32.6 us -> 30.8 us
    pallas_call x1, Pallas kernels: 32.1 us -> 30.3 us  [per_device(): pl.pallas_call(functools.partial(kernel, cfg), out_shape=jax.ShapeDtypeSt...]
where the time goes in v3:
time: 33.7 us; the launch traced here: 33.4 us
  Pallas kernels  30.8 us (91%)
  between operations  1.94 us (6%)
  local copies, waits for them, and re-layouts  0.66 us (2%)
    pallas_call x1, Pallas kernels, per_device(): pl.pallas_call(functools.partial(kernel, cfg), out_shape=jax.ShapeDtypeSt...  30.3 us

profile of v3, /device:TPU:0, one launch (start us, length us, event | category | flops | bytes accessed | tf_op | source)
XLA Modules:
  0.0 33.4 jit_solution(3305033297655355515)
XLA Ops:
  1.9 30.3 %shard_map.94.total = f32[8,128]{1,0:T(8,128)} custom-call(f32[6,12,2,128]{3,2,1,0:T(2,128)} %bitcast.3, s32[2,64]{1,0:T(2,128)} %row_hbm.1, s32[2,64]{1,0:T(2,128)} %col_hbm.1, f32[4]{0:T(128)} %lambdas_hbm.1, f32[1]{0:T(128)S(6)} %copy.10.inverse_temp, s32[1]{0:T(128)S(6)} %copy.11.parity, s32[4]{0:T(128)} %thresholds_hbm.1), custom_call_target="tpu_custom_call" | custom-call | tf_op jit(solution)/shard_map/pallas_call | solution.py:692
  32.2 0.0 copy-start
  32.2 0.7 %copy-done = f32[8,128]{1,0:T(8,128)S(1)} copy-done((f32[8,128]{1,0:T(8,128)S(1)}, f32[8,128]{1,0:T(8,128)}, u32[]{:S(2)}) %copy-start) | copy-done | bytes 4120
  32.9 0.6 %shard_map.95 = (f32[2,3]{1,0:T(2,128)}, f32[2]{0:T(128)}, f32[2]{0:T(128)}) custom-call(f32[8,128]{1,0:T(8,128)S(1)} %copy-done), custom_call_target="tpu_custom_call" | custom-call | tf_op jit(solution)/shard_map/pallas_call | solution.py:707
Async XLA Ops:
  32.2 0.7 %copy-start = (f32[8,128]{1,0:T(8,128)S(1)}, f32[8,128]{1,0:T(8,128)}, u32[]{:S(2)}) copy-start(f32[8,128]{1,0:T(8,128)} %shard_map.94.total) | copy-start | bytes 12292

commit v4 on v3

--- a/solution.py
+++ b/solution.py
@@ -1,4 +1,5 @@
 import functools
+import itertools
 
 import jax
 import jax.numpy as jnp
@@ -13,6 +14,7 @@
 PIECES = TILE // ROWS
 UNROLL = 4
 SPREAD = 4
+HEAD = 3
 LINES = 40
 LIMIT = 67043328
 MESH = pl.DeviceIdType.MESH
@@ -45,6 +47,10 @@
 
 def near_steps(dims):
     return min(2, dims[0])
+
+
+def backward(count):
+    return range(count - 1, -1, -1)
 
 
 def slots_of(groups, listed):
@@ -433,7 +439,7 @@
         lams = lambda_list(slot)
         softs = [2.0 - lam for lam in lams]
         count = fields_of(slot)
-        unroll = max(u for u in (1, 2, UNROLL) if (last - first) % u == 0)
+        unroll = max(u for u in (1, 2, UNROLL, 5, 8, 10) if (last - first) % u == 0)
 
         def pair_sum(pair, state):
             word = order[slot, pair]
@@ -546,23 +552,23 @@
     for slot in range(1, run):
         first_step = dim_z - 1 if slot == 1 and dim_z > 2 else 1
         later += [functools.partial(answer, slot, step) for step in range(first_step, dim_z)]
-    partial = []
-    for slot in range(run):
-        state = start_state(slot)
-        first = 0
-        for phase, end in enumerate(ends):
-            complete(slot, phase)
-            if slot == 0 and phase == len(ends) - 1:
-                for partner in partners:
-                    pl.semaphore_signal(ready, inc=1, device_id=partner, device_id_type=MESH)
-            if end > first:
-                state = tiles(slot, phase, first, end, state)
-            first = end
-            if slot == 0 and later:
+    turns = [(slot, phase) for slot in range(run) for phase in range(len(ends))]
+    if run == 2 and len(ends) > 2:
+        turns.sort(key=lambda turn: (turn[1] + HEAD * turn[0], turn[0]))
+    states = [start_state(slot) for slot in range(run)]
+    for slot, phase in turns:
+        complete(slot, phase)
+        if slot == 0 and phase == len(ends) - 1:
+            for partner in partners:
+                pl.semaphore_signal(ready, inc=1, device_id=partner, device_id_type=MESH)
+        first = ends[phase - 1] if phase else 0
+        if ends[phase] > first:
+            states[slot] = tiles(slot, phase, first, ends[phase], states[slot])
+        if later:
+            later.pop(0)()
+            while slot == 0 and phase == len(ends) - 1 and later:
                 later.pop(0)()
-        while later:
-            later.pop(0)()
-        partial.append(close(slot, state))
+    partial = [close(slot, states[slot]) for slot in range(run)]
 
     lane = lax.broadcasted_iota(jnp.int32, (1, TILE), 1)
     line = jnp.zeros((1, TILE), jnp.float32)
@@ -574,10 +580,10 @@
     for _ in partners:
         pl.semaphore_wait(ready, 1)
     everyone = wins * groups
-    for other_win in range(wins):
-        for step in range(groups):
-            if other_win or step:
-                target = ((win + other_win) % wins, (grp + step) % groups)
+    for step in range(dim_z - 1, -1, -1):
+        for dy, dx, other_win in itertools.product(*map(backward, (dim_y, dim_x, wins))):
+            if step or dy or dx or other_win:
+                target = ((win + other_win) % wins, group_at(plane_to(step), dy, dx))
                 pltpu.make_async_remote_copy(
                     src_ref=red.at[me],
                     dst_ref=red.at[me],

time: 33.7 us -> 33.3 us (0.988)
  Pallas kernels: 30.8 us -> 30.4 us
    pallas_call x1, Pallas kernels: 30.3 us -> 29.9 us  [per_device(): pl.pallas_call(functools.partial(kernel, cfg), out_shape=jax.ShapeDtypeSt...]
where the time goes in v4:
time: 33.3 us; the launch traced here: 33 us
  Pallas kernels  30.4 us (91%)
  between operations  1.94 us (6%)
  local copies, waits for them, and re-layouts  0.66 us (2%)
    pallas_call x1, Pallas kernels, per_device(): pl.pallas_call(functools.partial(kernel, cfg), out_shape=jax.ShapeDtypeSt...  29.9 us

profile of v4, /device:TPU:0, one launch (start us, length us, event | category | flops | bytes accessed | tf_op | source)
XLA Modules:
  0.0 33.0 jit_solution(3069929904731989942)
XLA Ops:
  1.9 29.9 %shard_map.94.total = f32[8,128]{1,0:T(8,128)} custom-call(f32[6,12,2,128]{3,2,1,0:T(2,128)} %bitcast.3, s32[2,64]{1,0:T(2,128)} %row_hbm.1, s32[2,64]{1,0:T(2,128)} %col_hbm.1, f32[4]{0:T(128)} %lambdas_hbm.1, f32[1]{0:T(128)S(6)} %copy.10.inverse_temp, s32[1]{0:T(128)S(6)} %copy.11.parity, s32[4]{0:T(128)} %thresholds_hbm.1), custom_call_target="tpu_custom_call" | custom-call | tf_op jit(solution)/shard_map/pallas_call | solution.py:698
  31.8 0.0 copy-start
  31.8 0.7 %copy-done = f32[8,128]{1,0:T(8,128)S(1)} copy-done((f32[8,128]{1,0:T(8,128)S(1)}, f32[8,128]{1,0:T(8,128)}, u32[]{:S(2)}) %copy-start) | copy-done | bytes 4120
  32.5 0.6 %shard_map.95 = (f32[2,3]{1,0:T(2,128)}, f32[2]{0:T(128)}, f32[2]{0:T(128)}) custom-call(f32[8,128]{1,0:T(8,128)S(1)} %copy-done), custom_call_target="tpu_custom_call" | custom-call | tf_op jit(solution)/shard_map/pallas_call | solution.py:713
Async XLA Ops:
  31.8 0.7 %copy-start = (f32[8,128]{1,0:T(8,128)S(1)}, f32[8,128]{1,0:T(8,128)}, u32[]{:S(2)}) copy-start(f32[8,128]{1,0:T(8,128)} %shard_map.94.total) | copy-start | bytes 12292
